TPU v7x, 512 devices: a 8x2x16 block of a 8x8x16 slice. The times are simulated.
512 devices in a mesh: grp: 2 (over y), seq: 128 (over z, x), head: 2 (over core).
Axes of the slice: x: 8, y: 2, z: 16, core: 2. Of those that a mesh axis runs over, the one named last changes fastest.
The devices are a block of a 8x8x16 slice.
Arguments:
- key_cache: bfloat16 [4, 1024, 128, 1024], P('grp', ('seq', 'head')), parts along dimension 0, may hold values from -160 to 160, as said below
- value_cache: bfloat16 [4, 1024, 128, 1024], P('grp', ('seq', 'head')), parts along dimension 0, may hold values from -16 to 16, as said below
- query: bfloat16 [4, 4096], P('grp', 'head'), parts along dimension 0, may hold values from -48 to 48, as said below
- lengths: int32 [4], P('grp'), parts along dimension 0, may hold values from 128 to 131072, as said below
- block_map: int32 [4, 1024], P('grp'), parts along dimension 0, may hold values from 0 to 1023, each once within a row
Outputs:
- attended: bfloat16 [4, 4096], P('grp', 'head'), parts along dimension 0
There are 2 independent parts, one for each index of `grp`. A program takes and returns all parts, laid end to end along the dimension named above; each array names one. Nothing has to cross between parts.
Inputs may be any that keep to these rules, and one draw needn't show every extreme that they name: `lengths`: every length is a multiple of 128; in every draw some request has length 131072. `key_cache`: finite entries, drawn afresh for every request, block, token and channel. `value_cache`: finite entries, drawn afresh for every request, block, token and channel. `query`: finite entries, drawn afresh for every request, head and channel.
All inputs are finite; a program needn't handle non-finite values.
Results may differ from a plain program's by a relative error of at most 0.0055.
Values may be sent and summed in bfloat16 or wider, within the bound.
No kernel may reach another device: no remote copies, remote signals or barrier semaphores. Data moves between devices by JAX's collectives and lax.ppermute only.
A program may use at most 64 MiB of HBM per device.

v0:
```python
import jax
import jax.numpy as jnp
from jax import lax
from jax.sharding import Mesh
from jax.sharding import PartitionSpec as P

QH = 32
KVH = 8
HD = 128
BLK = 128
SEQ = ("seq_0", "seq_1")
SEQ_HEAD = ("seq_0", "seq_1", "head")


def all_in_one(shard, axis):
    leaves = jax.tree.leaves(shard)
    sequence = sorted(range(len(leaves)), key=lambda k: -leaves[k].size)
    width = (1, *leaves[sequence[0]].shape)[-1]
    lines = [
        jnp.pad(leaves[k].reshape(-1), (0, -leaves[k].size % width)).reshape(-1, width)
        for k in sequence
    ]
    both, at, found = (lax.all_gather(jnp.concatenate(lines), axis), 0, {})
    for k, line in zip(sequence, lines):
        share = both[:, at : at + len(line)].reshape(len(both), -1)
        found[k] = share[:, : leaves[k].size].reshape(-1, *leaves[k].shape)
        at += len(line)
    numbers = iter(range(len(leaves)))
    return jax.tree.map(lambda _: found[next(numbers)], shard)


def combined_by_axis(shard, axes, combine):
    for axis in axes:
        pieces = all_in_one(shard, axis)
        shard = jax.tree.map(lambda part: part[0], pieces)
        for k in range(1, lax.axis_size(axis)):
            shard = combine(shard, jax.tree.map(lambda part: part[k], pieces))
    return shard


def combine(earlier, later):
    top_new = jnp.maximum(earlier[0], later[0])
    factor_a = jnp.exp(earlier[0] - top_new)
    factor_b = jnp.exp(later[0] - top_new)
    total = earlier[1] * factor_a + later[1] * factor_b
    summed_values = earlier[2] * factor_a[..., None] + later[2] * factor_b[..., None]
    return (top_new, total, summed_values)


def partials(key_rows, value_rows, queries, live_blocks):
    batch_rows = key_rows.shape[0]
    slot_count = key_rows.shape[1]
    group_count = key_rows.shape[3] // HD
    token_count = slot_count * BLK
    key_flat = key_rows.reshape(batch_rows, token_count, group_count, HD)
    value_flat = value_rows.reshape(batch_rows, token_count, group_count, HD)
    query_heads = queries.reshape(batch_rows, group_count, QH // KVH, HD)
    logit_scores = jnp.einsum(
        "bgqd,btgd->bgqt", query_heads, key_flat, preferred_element_type=jnp.float32
    )
    logit_scores = logit_scores * (1.0 / HD**0.5)
    logit_scores = logit_scores.reshape(batch_rows, group_count, QH // KVH, slot_count, BLK)
    live_mask = live_blocks[:, None, None, :, None]
    row_top = jnp.max(jnp.where(live_mask, logit_scores, jnp.float32(-1e30)), axis=(3, 4))
    expo = jnp.where(live_mask, jnp.exp(logit_scores - row_top[..., None, None]), jnp.float32(0.0))
    total = jnp.sum(expo, axis=(3, 4))
    weights = expo.astype(jnp.bfloat16).reshape(batch_rows, group_count, QH // KVH, token_count)
    summed_values = jnp.einsum(
        "bgqt,btgd->bgqd", weights, value_flat, preferred_element_type=jnp.float32
    )
    return (row_top, total, summed_values)


def owned_live(block_map, lengths, position, count):
    owned_blocks = lax.dynamic_slice_in_dim(block_map, position * count, count, 1)
    return owned_blocks < (lengths // BLK)[:, None]


def on_device(key_cache, value_cache, query, lengths, block_map):
    batch_rows = key_cache.shape[0]
    width_here = query.shape[1]
    key_rows, value_rows = (
        lax.all_to_all(key_cache, "head", split_axis=3, concat_axis=1, tiled=True),
        lax.all_to_all(value_cache, "head", split_axis=3, concat_axis=1, tiled=True),
    )
    live_blocks = owned_live(block_map, lengths, lax.axis_index(SEQ), key_rows.shape[1])
    local = partials(key_rows, value_rows, query, live_blocks)
    row_top, total, summed_values = combined_by_axis(local, SEQ, combine)
    result = summed_values / total[..., None]
    return result.reshape(batch_rows, width_here).astype(jnp.bfloat16)


def solution(mesh):
    torus = Mesh(
        mesh.devices.reshape(mesh.shape["grp"], 16, 8, mesh.shape["head"]),
        ("grp", "seq_0", "seq_1", "head"),
    )
    placed = (
        P("grp", SEQ_HEAD, None, None),
        P("grp", SEQ_HEAD, None, None),
        P("grp", "head"),
        P("grp"),
        P("grp", None),
    )
    return jax.shard_map(
        on_device, mesh=torus, in_specs=placed, out_specs=P("grp", "head"), check_vma=False
    )
```

profile of v0, /device:TPU:80, one launch (start us, length us, event | category | flops | bytes accessed | tf_op | source)
XLA Modules:
  0.0 132.9 jit_solution(2421228417511749975)
XLA Ops:
  0.0 4.3 %copy.10 = bf16[2,4,128,1024]{2,1,0,3:T(4,128)(2,1)} copy(bf16[2,4,128,1024]{3,2,1,0:T(8,128)(2,1)} %param.5) | data formatting | bytes 4194304 | tf_op args[0]
  4.3 3.9 %all-to-all-start = ((bf16[2,4,128,1024]{2,1,0,3:T(4,128)(2,1)}), bf16[2,4,128,1024]{2,1,0,3:T(4,128)(2,1)S(1)}, u32[]{:S(2)}, u32[]{:S(2)}) async-start(bf16[2,4,128,1024]{2,1,0,3:T(4,128)(2,1)} %copy.10), calls=%async_computation | async-start | bytes 4194304 | tf_op jit(solution)/shard_map/all_to_all | solution.py:83
  8.3 0.8 dynamic-slice_compare_fusion
  9.0 0.1 broadcast_bitcast_fusion
  9.2 4.3 %copy.13 = bf16[2,4,128,1024]{2,1,0,3:T(4,128)(2,1)} copy(bf16[2,4,128,1024]{3,2,1,0:T(8,128)(2,1)} %param.6) | data formatting | bytes 4194304 | tf_op args[1]
  13.5 4.8 %all-to-all-start.1 = ((bf16[2,4,128,1024]{2,1,0,3:T(4,128)(2,1)}), bf16[2,4,128,1024]{2,1,0,3:T(4,128)(2,1)}, u32[]{:S(2)}, u32[]{:S(2)}) async-start(bf16[2,4,128,1024]{2,1,0,3:T(4,128)(2,1)} %copy.13), calls=%async_computation.1 | async-start | bytes 4194304 | tf_op jit(solution)/shard_map/all_to_all | solution.py:84
  18.3 3.0 %copy.11 = bf16[2,4,128,2,512]{4,2,1,3,0:T(8,128)(2,1)} copy(bf16[2,4,128,2,512]{2,1,0,4,3:T(4,128)(2,1)S(1)} %bitcast.574) | data formatting | bytes 4194304 | tf_op jit(solution)/shard_map/all_to_all | solution.py:83
  21.4 2.5 %reshape.1675 = bf16[2,1024,4,128]{3,2,1,0:T(4,128)(2,1)S(1)} reshape(bf16[2,2,4,128,512]{4,3,2,1,0:T(8,128)(2,1)} %bitcast.575) | data formatting | bytes 4194304 | tf_op jit(solution)/shard_map/reshape | solution.py:55
  23.9 0.7 select_reduce_fusion
  24.6 0.1 reshape.1678
  24.7 0.2 fusion.7
  25.0 0.1 reshape.1680
  25.0 3.0 %copy.14 = bf16[2,4,128,2,512]{4,2,1,3,0:T(8,128)(2,1)S(1)} copy(bf16[2,4,128,2,512]{2,1,0,4,3:T(4,128)(2,1)} %bitcast.2) | data formatting | bytes 4194304 | tf_op jit(solution)/shard_map/all_to_all | solution.py:84
  28.0 2.1 %reshape.1676 = bf16[2,1024,4,128]{3,2,1,0:T(4,128)(2,1)} reshape(bf16[2,2,4,128,512]{4,3,2,1,0:T(8,128)(2,1)S(1)} %bitcast.576) | data formatting | bytes 4194304 | tf_op jit(solution)/shard_map/reshape | solution.py:56
  30.1 2.1 %fusion = f32[2,4,4,128]{3,2,1,0:T(4,128)S(1)} fusion(bf16[2,1024,4,128]{3,2,1,0:T(4,128)(2,1)} %reshape.1676, f32[2,4,4,1024]{3,2,1,0:T(4,128)S(1)} %get-tuple-element.91, f32[2,4,4]{2,1,0:T(4,128)S(1)} %get-tuple-element.90, pred[2,1024]{1,0:T(4,128)(4,1)S(1)} %bitcast.619), kind=kOutput, calls=%fused_computation | convolution fusion | flops 8486912 | bytes 2246784 | tf_op jit(solution)/shard_map/bgqt,btgd->bgqd/dot_general | solution.py:68
  32.2 69.8 %all-gather.2 = f32[16,34,128]{2,1,0:T(8,128)S(1)} all-gather(f32[1,34,128]{2,1,0:T(8,128)S(1)} %maximum_bitcast_fusion), channel_id=2, replica_groups=mesh['grp'=2,'seq_0'=16,'seq_1'=8,'head'=2] {'seq_0'}, dimensions={0}, use_global_device_ids=true | all-gather | bytes 295936 | tf_op jit(solution)/shard_map/all_gather | solution.py:23
  102.2 0.2 fusion.14
  102.4 26.6 %all-gather.3 = f32[8,34,128]{2,1,0:T(8,128)S(1)} all-gather(f32[1,34,128]{2,1,0:T(8,128)S(1)} %maximum_bitcast_fusion.1), channel_id=3, replica_groups=mesh['grp'=2,'seq_0'=16,'seq_1'=8,'head'=2] {'seq_1'}, dimensions={0}, use_global_device_ids=true | all-gather | bytes 156672 | tf_op jit(solution)/shard_map/all_gather | solution.py:23
  129.1 0.1 squeeze.276
  129.2 0.1 squeeze.280
  129.3 0.1 squeeze.274
  129.3 0.1 squeeze.272
  129.4 0.1 squeeze.270
  129.5 0.1 squeeze.268
  129.6 0.1 squeeze.266
  129.7 0.1 squeeze.265
  129.8 0.1 squeeze.278
  129.9 0.1 squeeze.287
  130.0 0.1 squeeze.286
  130.1 0.1 squeeze.285
  130.1 0.1 squeeze.284
  130.2 0.1 squeeze.283
  130.3 0.1 squeeze.282
  130.4 0.1 squeeze.281
  130.6 0.1 mul.784
  130.7 0.1 mul.787
  130.8 0.1 mul.781
  130.9 0.1 mul.778
  131.0 0.1 mul.775
  131.1 0.1 mul.772
  131.2 0.1 mul.769
  131.3 0.1 mul.766
  131.4 0.1 mul.763
  131.5 0.1 mul.760
  131.6 0.1 mul.757
  131.7 0.1 mul.754
  132.0 0.1 div.27
  132.2 0.7 fusion.58
  (48 shorter events, 0.9 us)
Async XLA Ops:
  4.3 3.9 %copy-start.1 = (s32[2]{0:T(128)S(1)}, s32[2]{0:T(128)}, u32[]{:S(2)}) copy-start(s32[2]{0:T(128)} %param.8) | copy-start | bytes 28
  4.3 4.8 %copy-start = (bf16[2,2048]{1,0:T(2,128)(2,1)S(1)}, bf16[2,2048]{1,0:T(2,128)(2,1)}, u32[]{:S(2)}) copy-start(bf16[2,2048]{1,0:T(2,128)(2,1)} %param.7) | copy-start | bytes 24580
  4.3 9.1 %all-to-all-start = ((bf16[2,4,128,1024]{2,1,0,3:T(4,128)(2,1)}), bf16[2,4,128,1024]{2,1,0,3:T(4,128)(2,1)S(1)}, u32[]{:S(2)}, u32[]{:S(2)}) async-start(bf16[2,4,128,1024]{2,1,0,3:T(4,128)(2,1)} %copy.10), calls=%async_computation | async-start | bytes 4194304 | tf_op jit(solution)/shard_map/all_to_all | solution.py:83
  13.5 11.6 %all-to-all-start.1 = ((bf16[2,4,128,1024]{2,1,0,3:T(4,128)(2,1)}), bf16[2,4,128,1024]{2,1,0,3:T(4,128)(2,1)}, u32[]{:S(2)}, u32[]{:S(2)}) async-start(bf16[2,4,128,1024]{2,1,0,3:T(4,128)(2,1)} %copy.13), calls=%async_computation.1 | async-start | bytes 4194304 | tf_op jit(solution)/shard_map/all_to_all | solution.py:84
where the time goes:
time: 133 us
  blocking collectives  96.4 us (72%)
  local copies, waits for them, and re-layouts  22.6 us (17%)
  starting transfers between devices  8.77 us (7%)
  matrix products  2.8 us (2%)
  other arithmetic  2.06 us (2%)
    all_gather x2, blocking collectives, all_in_one(): both, at, found = (lax.all_gather(jnp.concatenate(lines), axis), 0, {})  96.4 us
    unnamed x8, local copies, waits for them, and re-layouts  8.7 us
    all_to_all x1, starting transfers between devices, on_device(): lax.all_to_all(value_cache, 'head', split_axis=3, concat_axis=1, tiled=True)  4.84 us
    all_to_all x1, starting transfers between devices, on_device(): lax.all_to_all(key_cache, 'head', split_axis=3, concat_axis=1, tiled=True)  3.92 us
    all_to_all x1, local copies, waits for them, and re-layouts, on_device(): lax.all_to_all(key_cache, 'head', split_axis=3, concat_axis=1, tiled=True)  3.04 us
    all_to_all x1, local copies, waits for them, and re-layouts, on_device(): lax.all_to_all(value_cache, 'head', split_axis=3, concat_axis=1, tiled=True)  2.98 us
  transfers between devices with their start and end apart: 2, of which 0 were waited for; matrix products, arithmetic and copies ran while one was open for 9% of the time, Pallas kernels for 0%

commit v1 on v0

v1 whole, which is shorter than its diff:
```python
import jax
import jax.numpy as jnp
from jax import lax
from jax.experimental import pallas as pl
from jax.experimental.pallas import tpu as pltpu
from jax.sharding import Mesh
from jax.sharding import PartitionSpec as P

QH = 32
KVH = 8
HD = 128
BLK = 128
GROUP = QH // KVH
LOW = -1e30
ROW = ("seq_1", "head")
STATS = 8


def pieces(x):
    first = x.astype(jnp.bfloat16)
    rest = x - first.astype(jnp.float32)
    second = rest.astype(jnp.bfloat16)
    third = (rest - second.astype(jnp.float32)).astype(jnp.bfloat16)
    return first, second, third


def diagonal(rows):
    shape = (rows, HD)
    return lax.broadcasted_iota(jnp.int32, shape, 0) == lax.broadcasted_iota(jnp.int32, shape, 1)


def as_row(column, eye):
    return jnp.sum(jnp.where(eye, column, 0.0), axis=0, keepdims=True)


def as_column(row, eye):
    return jnp.sum(jnp.where(eye, row, 0.0), axis=1, keepdims=True)


def packed(sums, top, total):
    blank = jnp.zeros((STATS - 6, HD), jnp.float32)
    stats = [p.astype(jnp.float32) for p in (*pieces(top), *pieces(total))]
    return jnp.concatenate([sums, *stats, blank], axis=0).astype(jnp.bfloat16)


def attend_kernel(query, lengths, block_map, keys, values, out, key_buf, value_buf, map_buf, len_buf, sems):
    batch, slots = keys.shape[0], keys.shape[1]
    halves = query.shape[0]
    tokens = slots * BLK
    width = keys.shape[3]
    copies = []
    for b in range(batch):
        copies.append(
            (
                pltpu.make_async_copy(keys.at[b], key_buf.at[b], sems.at[0, b]),
                pltpu.make_async_copy(values.at[b], value_buf.at[b], sems.at[1, b]),
            )
        )
    small = (
        pltpu.make_async_copy(block_map, map_buf, sems.at[2, 0]),
        pltpu.make_async_copy(lengths, len_buf, sems.at[2, 1]),
    )
    for copy in small:
        copy.start()
    for pair in copies:
        for copy in pair:
            copy.start()
    for copy in small:
        copy.wait()
    first = lax.axis_index(("seq_0", "seq_1", "head")) * slots
    row_group = lax.broadcasted_iota(jnp.int32, (KVH, width), 0)
    column_group = lax.broadcasted_iota(jnp.int32, (KVH, width), 1) // HD
    own = row_group == column_group
    eye = diagonal(batch * QH // halves)
    sums, tops, totals = [], [], []
    for b in range(batch):
        spread = []
        for i in range(GROUP):
            chunks = []
            for g in range(KVH):
                half, at = divmod(g * GROUP + i, QH // halves)
                chunks.append(query[half, b : b + 1, at * HD : (at + 1) * HD].astype(jnp.float32))
            line = jnp.concatenate(chunks, axis=1)
            spread.append(jnp.where(own, line, 0.0))
        spread = jnp.concatenate(spread, axis=0).astype(jnp.bfloat16)
        limit = len_buf[b] // BLK
        live = jnp.concatenate(
            [
                jnp.full((1, BLK), (map_buf[b, first + j] < limit).astype(jnp.int32))
                for j in range(slots)
            ],
            axis=1,
        )
        live = jnp.broadcast_to(live, (QH, tokens)) > 0
        copies[b][0].wait()
        scores = lax.dot_general(
            spread,
            key_buf[b].reshape(tokens, width),
            (((1,), (1,)), ((), ())),
            preferred_element_type=jnp.float32,
        )
        scores = jnp.where(live, scores * (1.0 / HD**0.5), LOW)
        top = jnp.max(scores, axis=1, keepdims=True)
        expo = jnp.where(live, jnp.exp(scores - top), 0.0)
        total = jnp.sum(expo, axis=1, keepdims=True)
        copies[b][1].wait()
        wide = jnp.dot(
            expo.astype(jnp.bfloat16),
            value_buf[b].reshape(tokens, width),
            preferred_element_type=jnp.float32,
        )
        wide = wide.reshape(GROUP, KVH, width)
        mine = jnp.zeros((GROUP, KVH, HD), jnp.float32)
        for g in range(KVH):
            pick = lax.broadcasted_iota(jnp.int32, mine.shape, 1) == g
            mine = jnp.where(pick, wide[:, :, g * HD : (g + 1) * HD], mine)
        sums.append(mine)
        tops.append(top.reshape(GROUP, KVH, 1))
        totals.append(total.reshape(GROUP, KVH, 1))
    per = KVH // halves
    for half in range(halves):
        part = slice(half * per, (half + 1) * per)

        def gathered(arrays):
            return jnp.concatenate([a[i : i + 1, part].reshape(per, -1) for a in arrays for i in range(GROUP)], axis=0)

        line = packed(
            gathered(sums),
            as_row(gathered(tops), eye),
            as_row(gathered(totals), eye),
        )
        for k in range(out.shape[0]):
            out[k, half] = line


def combined(parts):
    count, rows = parts.shape[0], parts.shape[1] - STATS
    eye = diagonal(rows)
    stats = [parts[:, rows + k, :].astype(jnp.float32) for k in range(6)]
    tops = stats[0] + stats[1] + stats[2]
    totals = stats[3] + stats[4] + stats[5]
    top = jnp.max(tops, axis=0, keepdims=True)
    factors = jnp.exp(tops - top)
    total = jnp.sum(totals * factors, axis=0, keepdims=True)
    sums = jnp.zeros((rows, HD), jnp.float32)
    for n in range(count):
        sums += as_column(factors[n : n + 1], eye) * parts[n, :rows, :].astype(jnp.float32)
    return sums, top, total


def middle_kernel(parts, out):
    line = packed(*combined(parts))
    for k in range(out.shape[0]):
        out[k] = line


def last_kernel(parts, out):
    rows = parts.shape[1] - STATS
    batch = out.shape[0]
    per = rows // batch // GROUP
    sums, _, total = combined(parts)
    total = as_column(total, diagonal(rows))
    result = sums / total
    lines = []
    for b in range(batch):
        at = [b * per * GROUP + i * per + g for g in range(per) for i in range(GROUP)]
        lines.append(jnp.concatenate([result[r : r + 1] for r in at], axis=1))
    out[...] = jnp.concatenate(lines, axis=0).astype(out.dtype)


def on_device(key_cache, value_cache, query, lengths, block_map):
    batch, slots, _, width = key_cache.shape
    row_count, column_count = lax.axis_size("seq_0"), lax.axis_size("seq_1")
    halves = lax.axis_size("head")
    rows = batch * QH // halves + STATS
    anywhere = pl.BlockSpec(memory_space=pl.ANY)
    queries = lax.all_gather(query, "head")
    local = pl.pallas_call(
        attend_kernel,
        out_shape=jax.ShapeDtypeStruct((column_count, halves, rows, HD), jnp.bfloat16),
        in_specs=[pl.BlockSpec(memory_space=pltpu.VMEM), anywhere, anywhere, anywhere, anywhere],
        scratch_shapes=[
            pltpu.VMEM(key_cache.shape, key_cache.dtype),
            pltpu.VMEM(value_cache.shape, value_cache.dtype),
            pltpu.SMEM(block_map.shape, block_map.dtype),
            pltpu.SMEM(lengths.shape, lengths.dtype),
            pltpu.SemaphoreType.DMA((3, 2)),
        ],
        name="attend",
    )(queries, lengths, block_map, key_cache, value_cache)
    parts = local.reshape(column_count * halves, rows, HD)
    parts = lax.all_to_all(parts, ROW, 0, 0, tiled=True)
    parts = pl.pallas_call(
        middle_kernel,
        out_shape=jax.ShapeDtypeStruct((row_count, rows, HD), jnp.bfloat16),
        name="middle",
    )(parts)
    parts = lax.all_to_all(parts, "seq_0", 0, 0, tiled=True)
    return pl.pallas_call(
        last_kernel,
        out_shape=jax.ShapeDtypeStruct(query.shape, query.dtype),
        name="last",
    )(parts)


def solution(mesh):
    torus = Mesh(
        mesh.devices.reshape(mesh.shape["grp"], 16, 8, mesh.shape["head"]),
        ("grp", "seq_0", "seq_1", "head"),
    )
    cache = P("grp", ("seq_0", "seq_1", "head"), None, None)
    placed = (cache, cache, P("grp", "head"), P("grp"), P("grp", None))
    return jax.shard_map(
        on_device, mesh=torus, in_specs=placed, out_specs=P("grp", "head"), check_vma=False
    )
```

time: 133 us -> 86.6 us (0.65)
  local copies, waits for them, and re-layouts: 22.6 us -> 0 us
  blocking collectives: 96.4 us -> 78.2 us
  starting transfers between devices: 8.77 us -> 0 us
  Pallas kernels: 0 us -> 7.89 us
  matrix products: 2.8 us -> 0 us
  other arithmetic: 2.06 us -> 0 us
    all_gather x2 -> x1, blocking collectives: 96.4 us -> 3.13 us  [on_device(): queries = lax.all_gather(query, 'head')]
    all_to_all x0 -> x2, blocking collectives: none -> 75 us  [the longest x1 58.3 us: on_device(): parts = lax.all_to_all(parts, 'seq_0', 0, 0, tiled=True)]
    all_to_all x2 -> x0, starting transfers between devices: 8.77 us -> none  [the longest x1 4.84 us: on_device(): lax.all_to_all(value_cache, 'head', split_axis=3, concat_axis=1, tiled=True)]
    unnamed x8 -> x0, local copies, waits for them, and re-layouts: 8.7 us -> none
    pallas_call x0 -> x3, Pallas kernels: none -> 7.89 us  [the longest x1 4.43 us: on_device(): pl.pallas_call(attend_kernel, out_shape=jax.ShapeDtypeStruct((column_coun...]
    all_to_all x2 -> x0, local copies, waits for them, and re-layouts: 6.02 us -> none  [the longest x1 3.04 us: on_device(): lax.all_to_all(key_cache, 'head', split_axis=3, concat_axis=1, tiled=True)]
    reshape x8 -> x0, local copies, waits for them, and re-layouts: 4.84 us -> none  [the longest x1 2.55 us: partials(): key_flat = key_rows.reshape(batch_rows, token_count, group_count, HD)]
    dot_general x2 -> x0, matrix products: 2.8 us -> none  [the longest x1 2.06 us: partials(): jnp.einsum('bgqt,btgd->bgqd', weights, value_flat, preferred_element_type...]
  transfers between devices with their start and end apart: 2 -> 0, of which waited for: 0 -> 0; matrix products, arithmetic and copies ran while one was open for 9% -> 0% of each run, Pallas kernels for 0% -> 0%
where the time goes in v1:
time: 86.6 us; the launch traced here: 86.1 us
  blocking collectives  78.2 us (90%)
  Pallas kernels  7.89 us (9%)
    all_to_all x1, blocking collectives, on_device(): parts = lax.all_to_all(parts, 'seq_0', 0, 0, tiled=True)  58.3 us
    all_to_all x1, blocking collectives, on_device(): parts = lax.all_to_all(parts, ROW, 0, 0, tiled=True)  16.7 us
    pallas_call x1, Pallas kernels, on_device(): pl.pallas_call(attend_kernel, out_shape=jax.ShapeDtypeStruct((column_coun...  4.43 us
    all_gather x1, blocking collectives, on_device(): queries = lax.all_gather(query, 'head')  3.13 us
    pallas_call x1, Pallas kernels, on_device(): pl.pallas_call(middle_kernel, out_shape=jax.ShapeDtypeStruct((row_count,...  1.76 us

profile of v1, /device:TPU:80, one launch (start us, length us, event | category | flops | bytes accessed | tf_op | source)
XLA Modules:
  0.0 86.1 jit_solution(17895520295569897742)
XLA Ops:
  0.0 3.1 %all-gather.1.query = bf16[2,2,2048]{2,1,0:T(2,128)(2,1)} all-gather(bf16[1,2,2048]{2,1,0:T(2,128)(2,1)} %bitcast.3), channel_id=2, replica_groups=mesh['grp'=2,'seq_0'=16,'seq_1'=8,'head'=2] {'head'}, dimensions={0}, use_global_device_ids=true | all-gather | bytes 24576 | tf_op jit(solution)/shard_map/all_gather | solution.py:177
  3.1 4.4 %attend.1 = bf16[8,2,40,128]{3,2,1,0:T(8,128)(2,1)} custom-call(bf16[2,2,2048]{2,1,0:T(2,128)(2,1)} %all-gather.1.query, s32[2]{0:T(128)} %lengths.1, s32[2,1024]{1,0:T(2,128)} %block_map.1, bf16[2,4,128,1024]{3,2,1,0:T(8,128)(2,1)} %keys.1, bf16[2,4,128,1024]{3,2,1,0:T(8,128)(2,1)} %values.1), custom_call_target="tpu_custom_call" | custom-call | tf_op jit(solution)/shard_map/attend/pallas_call | solution.py:178
  7.6 16.7 %all_to_all.10.parts = bf16[16,40,128]{2,1,0:T(8,128)(2,1)} all-to-all(bf16[16,40,128]{2,1,0:T(8,128)(2,1)} %bitcast.2), channel_id=1, replica_groups=mesh['grp'=2,'seq_0'=16,'seq_1'=8,'head'=2] {'seq_1','head'}, dimensions={0} | all-to-all | bytes 327680 | tf_op jit(solution)/shard_map/all_to_all | solution.py:192
  24.3 1.8 %middle.1 = bf16[16,40,128]{2,1,0:T(8,128)(2,1)} custom-call(bf16[16,40,128]{2,1,0:T(8,128)(2,1)} %all_to_all.10.parts), custom_call_target="tpu_custom_call" | custom-call | tf_op jit(solution)/shard_map/middle/pallas_call | solution.py:193
  26.1 58.3 %all_to_all.11.parts = bf16[16,40,128]{2,1,0:T(8,128)(2,1)} all-to-all(bf16[16,40,128]{2,1,0:T(8,128)(2,1)} %middle.1), channel_id=1, replica_groups=mesh['grp'=2,'seq_0'=16,'seq_1'=8,'head'=2] {'seq_0'}, dimensions={0} | all-to-all | bytes 327680 | tf_op jit(solution)/shard_map/all_to_all | solution.py:198
  84.4 1.7 %last.1 = bf16[2,2048]{1,0:T(2,128)(2,1)} custom-call(bf16[16,40,128]{2,1,0:T(8,128)(2,1)} %all_to_all.11.parts), custom_call_target="tpu_custom_call" | custom-call | tf_op jit(solution)/shard_map/last/pallas_call | solution.py:199

commit v2 on v1

--- a/solution.py
+++ b/solution.py
@@ -168,6 +168,10 @@
     out[...] = jnp.concatenate(lines, axis=0).astype(out.dtype)
 
 
+def near(x):
+    return pltpu.with_memory_space_constraint(x, pltpu.VMEM)
+
+
 def on_device(key_cache, value_cache, query, lengths, block_map):
     batch, slots, _, width = key_cache.shape
     row_count, column_count = lax.axis_size("seq_0"), lax.axis_size("seq_1")
@@ -177,7 +181,7 @@
     queries = lax.all_gather(query, "head")
     local = pl.pallas_call(
         attend_kernel,
-        out_shape=jax.ShapeDtypeStruct((column_count, halves, rows, HD), jnp.bfloat16),
+        out_shape=pltpu.VMEM((column_count, halves, rows, HD), jnp.bfloat16),
         in_specs=[pl.BlockSpec(memory_space=pltpu.VMEM), anywhere, anywhere, anywhere, anywhere],
         scratch_shapes=[
             pltpu.VMEM(key_cache.shape, key_cache.dtype),
@@ -187,20 +191,20 @@
             pltpu.SemaphoreType.DMA((3, 2)),
         ],
         name="attend",
-    )(queries, lengths, block_map, key_cache, value_cache)
+    )(near(queries), lengths, block_map, key_cache, value_cache)
     parts = local.reshape(column_count * halves, rows, HD)
     parts = lax.all_to_all(parts, ROW, 0, 0, tiled=True)
     parts = pl.pallas_call(
         middle_kernel,
-        out_shape=jax.ShapeDtypeStruct((row_count, rows, HD), jnp.bfloat16),
+        out_shape=pltpu.VMEM((row_count, rows, HD), jnp.bfloat16),
         name="middle",
-    )(parts)
+    )(near(parts))
     parts = lax.all_to_all(parts, "seq_0", 0, 0, tiled=True)
     return pl.pallas_call(
         last_kernel,
         out_shape=jax.ShapeDtypeStruct(query.shape, query.dtype),
         name="last",
-    )(parts)
+    )(near(parts))
 
 
 def solution(mesh):

time: 86.6 us -> 80.7 us (0.932)
  Pallas kernels: 7.89 us -> 4.04 us
  blocking collectives: 78.2 us -> 76.5 us
    pallas_call x2, Pallas kernels: 6.18 us -> 3.25 us  [the longest x1 3.06 us: on_device(): pl.pallas_call(attend_kernel, out_shape=pltpu.VMEM((column_count, halves,...]
    all_gather x1, blocking collectives: 3.13 us -> 2.05 us  [on_device(): queries = lax.all_gather(query, 'head')]
    pallas_call x1, Pallas kernels: 1.71 us -> 0.79 us  [on_device(): pl.pallas_call(last_kernel, out_shape=jax.ShapeDtypeStruct(query.shape, q...]
where the time goes in v2:
time: 80.7 us; the launch traced here: 80.5 us
  blocking collectives  76.5 us (95%)
  Pallas kernels  4.04 us (5%)
    all_to_all x1, blocking collectives, on_device(): parts = lax.all_to_all(parts, 'seq_0', 0, 0, tiled=True)  58 us
    all_to_all x1, blocking collectives, on_device(): parts = lax.all_to_all(parts, ROW, 0, 0, tiled=True)  16.4 us
    pallas_call x1, Pallas kernels, on_device(): pl.pallas_call(attend_kernel, out_shape=pltpu.VMEM((column_count, halves,...  3.06 us
    all_gather x1, blocking collectives, on_device(): queries = lax.all_gather(query, 'head')  2.05 us

profile of v2, /device:TPU:80, one launch (start us, length us, event | category | flops | bytes accessed | tf_op | source)
XLA Modules:
  0.0 80.5 jit_solution(14072894305834131780)
XLA Ops:
  0.0 2.0 %all-gather.1.query = bf16[2,2,2048]{2,1,0:T(2,128)(2,1)S(1)} all-gather(bf16[1,2,2048]{2,1,0:T(2,128)(2,1)} %bitcast.3), channel_id=2, replica_groups=mesh['grp'=2,'seq_0'=16,'seq_1'=8,'head'=2] {'head'}, dimensions={0}, use_global_device_ids=true | all-gather | bytes 24576 | tf_op jit(solution)/shard_map/all_gather | solution.py:181
  2.0 3.1 %attend.1 = bf16[8,2,40,128]{3,2,1,0:T(8,128)(2,1)S(1)} custom-call(bf16[2,2,2048]{2,1,0:T(2,128)(2,1)S(1)} %all-gather.1.query, s32[2]{0:T(128)} %lengths.1, s32[2,1024]{1,0:T(2,128)} %block_map.1, bf16[2,4,128,1024]{3,2,1,0:T(8,128)(2,1)} %keys.1, bf16[2,4,128,1024]{3,2,1,0:T(8,128)(2,1)} %values.1), custom_call_target="tpu_custom_call" | custom-call | tf_op jit(solution)/shard_map/attend/pallas_call | solution.py:182
  5.1 16.4 %all_to_all.10.parts = bf16[16,40,128]{2,1,0:T(8,128)(2,1)S(1)} all-to-all(bf16[16,40,128]{2,1,0:T(8,128)(2,1)S(1)} %bitcast.2), channel_id=1, replica_groups=mesh['grp'=2,'seq_0'=16,'seq_1'=8,'head'=2] {'seq_1','head'}, dimensions={0} | all-to-all | bytes 327680 | tf_op jit(solution)/shard_map/all_to_all | solution.py:196
  21.5 0.2 middle.1
  21.7 58.0 %all_to_all.11.parts = bf16[16,40,128]{2,1,0:T(8,128)(2,1)S(1)} all-to-all(bf16[16,40,128]{2,1,0:T(8,128)(2,1)S(1)} %middle.1), channel_id=1, replica_groups=mesh['grp'=2,'seq_0'=16,'seq_1'=8,'head'=2] {'seq_0'}, dimensions={0} | all-to-all | bytes 327680 | tf_op jit(solution)/shard_map/all_to_all | solution.py:202
  79.7 0.8 last.1

commit v3 on v2

--- a/solution.py
+++ b/solution.py
@@ -1,3 +1,5 @@
+import functools
+
 import jax
 import jax.numpy as jnp
 from jax import lax
@@ -133,14 +135,23 @@
             out[k, half] = line
 
 
-def combined(parts):
+def combined(parts, held=None):
     count, rows = parts.shape[0], parts.shape[1] - STATS
     eye = diagonal(rows)
     stats = [parts[:, rows + k, :].astype(jnp.float32) for k in range(6)]
     tops = stats[0] + stats[1] + stats[2]
     totals = stats[3] + stats[4] + stats[5]
+    if held is not None:
+        place = lax.broadcasted_iota(jnp.int32, tops.shape, 0)
+        counted = place < 0
+        for n in range(count):
+            counted |= (place == n) & held[n]
+        tops = jnp.where(counted, tops, LOW)
+        totals = jnp.where(counted, totals, 0.0)
     top = jnp.max(tops, axis=0, keepdims=True)
     factors = jnp.exp(tops - top)
+    if held is not None:
+        factors = jnp.where(counted, factors, 0.0)
     total = jnp.sum(totals * factors, axis=0, keepdims=True)
     sums = jnp.zeros((rows, HD), jnp.float32)
     for n in range(count):
@@ -149,9 +160,19 @@
 
 
 def middle_kernel(parts, out):
-    line = packed(*combined(parts))
-    for k in range(out.shape[0]):
-        out[k] = line
+    out[...] = packed(*combined(parts))
+
+
+def merge_kernel(*refs, receivers):
+    *parts, out = refs
+    row = lax.axis_index("seq_0")
+    held = [row >= 0]
+    for rows in receivers:
+        got = row < 0
+        for r in rows:
+            got |= row == r
+        held.append(got)
+    out[...] = packed(*combined(jnp.stack([p[...] for p in parts]), held))
 
 
 def last_kernel(parts, out):
@@ -192,19 +213,49 @@
         ],
         name="attend",
     )(near(queries), lengths, block_map, key_cache, value_cache)
+    row, n = lax.axis_index("seq_0"), row_count
+    early, inside, outer = (row >= 1) & (row < n - 4), (row < 4) | (row >= n - 4), row >= 4
+    local, row, early, inside, outer = lax.optimization_barrier((local, row, early, inside, outer))
     parts = local.reshape(column_count * halves, rows, HD)
     parts = lax.all_to_all(parts, ROW, 0, 0, tiled=True)
-    parts = pl.pallas_call(
-        middle_kernel,
-        out_shape=pltpu.VMEM((row_count, rows, HD), jnp.bfloat16),
-        name="middle",
-    )(near(parts))
-    parts = lax.all_to_all(parts, "seq_0", 0, 0, tiled=True)
-    return pl.pallas_call(
-        last_kernel,
-        out_shape=jax.ShapeDtypeStruct(query.shape, query.dtype),
-        name="last",
-    )(near(parts))
+    parts, row, early, inside, outer = lax.optimization_barrier((parts, row, early, inside, outer))
+    line = pltpu.VMEM((rows, HD), jnp.bfloat16)
+    own = pl.pallas_call(middle_kernel, out_shape=line, name="middle")(near(parts))
+    hub = [(n - 4 + k) % n for k in range(8)]
+    outside = [r for r in range(n) if r not in hub]
+
+    def merged(receivers, *parts):
+        kernel = functools.partial(merge_kernel, receivers=receivers)
+        return pl.pallas_call(kernel, out_shape=line, name="merge")(*map(near, parts))
+
+    def moved(x, pairs):
+        return lax.ppermute(x, "seq_0", pairs)
+
+    def collected(own):
+        pairs = [(8, 7), (6, 5)]
+        own = merged([[b for _, b in pairs]], own, moved(own, pairs))
+        first, second = [(11, 3), (10, 2), (9, 1)], [(7, 3), (5, 2), (4, 1)]
+        to = [b for _, b in first]
+        return merged([to, to], own, moved(own, first), moved(own, second))
+
+    own = lax.cond(early, collected, lambda x: x, own)
+
+    def finished(own):
+        parts = jnp.broadcast_to(own[None], (len(hub), *own.shape))
+        parts = lax.all_to_all(parts, "seq_0", 0, 0, tiled=True, axis_index_groups=[hub, outside])
+        return pl.pallas_call(
+            last_kernel, out_shape=jax.ShapeDtypeStruct(query.shape, query.dtype), name="last"
+        )(near(parts))
+
+    result = lax.cond(inside, finished, lambda x: jnp.zeros(query.shape, query.dtype), own)
+
+    def spread(result):
+        near_pairs = [(15, 4), (14, 5), (13, 6), (12, 7)]
+        far_pairs = [(15, 8), (14, 9), (13, 10), (12, 11)]
+        first, second = moved(result, near_pairs), moved(result, far_pairs)
+        return jnp.where(row < 8, first, jnp.where(row < 12, second, result))
+
+    return lax.cond(outer, spread, lambda x: x, result)
 
 
 def solution(mesh):

time: 80.7 us -> 80 us (level)
  blocking collectives: 76.5 us -> 58.3 us
  waiting for transfers between devices: 0 us -> 8.99 us
  starting transfers between devices: 0 us -> 7.64 us
    all_to_all x2 -> x1, blocking collectives: 74.4 us -> 56.2 us  [finished(): lax.all_to_all(parts, 'seq_0', 0, 0, tiled=True, axis_index_groups=[hub,...]
    all_to_all x0 -> x1, waiting for transfers between devices: none -> 8.99 us  [on_device(): parts = lax.all_to_all(parts, ROW, 0, 0, tiled=True)]
    all_to_all x0 -> x1, starting transfers between devices: none -> 7.64 us  [on_device(): parts = lax.all_to_all(parts, ROW, 0, 0, tiled=True)]
  transfers between devices with their start and end apart: 0 -> 1, of which waited for: 0 -> 1; matrix products, arithmetic and copies ran while one was open for 0% -> 0% of each run, Pallas kernels for 0% -> 0%
where the time goes in v3:
time: 80 us; the launch traced here: 79.7 us
  blocking collectives  58.3 us (73%)
  waiting for transfers between devices  8.99 us (11%)
  starting transfers between devices  7.64 us (10%)
  Pallas kernels  4.04 us (5%)
    all_to_all x1, blocking collectives, finished(): lax.all_to_all(parts, 'seq_0', 0, 0, tiled=True, axis_index_groups=[hub,...  56.2 us
    all_to_all x1, waiting for transfers between devices, on_device(): parts = lax.all_to_all(parts, ROW, 0, 0, tiled=True)  8.99 us
    all_to_all x1, starting transfers between devices, on_device(): parts = lax.all_to_all(parts, ROW, 0, 0, tiled=True)  7.64 us
    pallas_call x1, Pallas kernels, on_device(): pl.pallas_call(attend_kernel, out_shape=pltpu.VMEM((column_count, halves,...  3.72 us
    all_gather x1, blocking collectives, on_device(): queries = lax.all_gather(query, 'head')  2.05 us
  transfers between devices with their start and end apart: 1, of which 1 were waited for; matrix products, arithmetic and copies ran while one was open for 0% of the time, Pallas kernels for 0%

profile of v3, /device:TPU:80, one launch (start us, length us, event | category | flops | bytes accessed | tf_op | source)
XLA Modules:
  0.0 79.7 jit_solution(5278945739929367656)
XLA Ops:
  0.0 2.0 %all-gather.1.query = bf16[2,2,2048]{2,1,0:T(2,128)(2,1)S(1)} all-gather(bf16[1,2,2048]{2,1,0:T(2,128)(2,1)} %bitcast.2), channel_id=2, replica_groups=mesh['grp'=2,'seq_0'=16,'seq_1'=8,'head'=2] {'head'}, dimensions={0}, use_global_device_ids=true | all-gather | bytes 24576 | tf_op jit(solution)/shard_map/all_gather | solution.py:202
  2.1 3.7 %attend.1 = bf16[8,2,40,128]{3,2,1,0:T(8,128)(2,1)} custom-call(bf16[2,2,2048]{2,1,0:T(2,128)(2,1)S(1)} %all-gather.1.query, s32[2]{0:T(128)} %lengths.1, s32[2,1024]{1,0:T(2,128)} %block_map.1, bf16[2,4,128,1024]{3,2,1,0:T(8,128)(2,1)} %keys.1, bf16[2,4,128,1024]{3,2,1,0:T(8,128)(2,1)} %values.1), custom_call_target="tpu_custom_call" | custom-call | tf_op jit(solution)/shard_map/attend/pallas_call | solution.py:203
  5.8 7.6 %all-to-all-start.1 = ((bf16[16,40,128]{2,1,0:T(8,128)(2,1)}), bf16[16,40,128]{2,1,0:T(8,128)(2,1)S(1)}, u32[]{:S(2)}, u32[]{:S(2)}) async-start(bf16[16,40,128]{2,1,0:T(8,128)(2,1)} %bitcast.1), calls=%async_computation.1 | async-start | bytes 327680 | tf_op jit(solution)/shard_map/all_to_all | solution.py:220
  13.4 9.0 %all-to-all-done.1.parts = bf16[16,40,128]{2,1,0:T(8,128)(2,1)S(1)} async-done(((bf16[16,40,128]{2,1,0:T(8,128)(2,1)}), bf16[16,40,128]{2,1,0:T(8,128)(2,1)S(1)}, u32[]{:S(2)}, u32[]{:S(2)}) %all-to-all-start.1) | async-done | bytes 163872 | tf_op jit(solution)/shard_map/all_to_all | solution.py:220
  22.4 0.2 middle.1
  22.6 56.4 %conditional.4 = (bf16[2,2048]{1,0:T(2,128)(2,1)S(1)}) conditional(s32[]{:T(128)} %convert_element_type.10, () %tuple.27, bf16[40,128]{1,0:T(8,128)(2,1)S(1)} %get-tuple-element.47), branch_computations={%region_2.0_spmd, %region_3.0_spmd} | conditional | bytes 256008 | solution.py:250
  22.7 56.2 %all_to_all.9.parts = bf16[8,40,128]{2,1,0:T(8,128)(2,1)S(1)} all-to-all(bf16[8,40,128]{2,1,0:T(8,128)(2,1)S(1)} %broadcast_in_dim.0), channel_id=1, replica_groups={{192,208,224,240,0,16,32,48},{64,80,96,112,128,144,160,176},{193,209,22..., dimensions={0} | all-to-all | bytes 163840 | tf_op jit(solution)/shard_map/cond/branch_1_fun/all_to_all | solution.py:245
  78.9 0.1 last.1
  79.1 0.0 copy-start
  79.1 0.6 copy-done
  (3 shorter events, 0.0 us)
Async XLA Ops:
  5.8 16.6 %all-to-all-start.1 = ((bf16[16,40,128]{2,1,0:T(8,128)(2,1)}), bf16[16,40,128]{2,1,0:T(8,128)(2,1)S(1)}, u32[]{:S(2)}, u32[]{:S(2)}) async-start(bf16[16,40,128]{2,1,0:T(8,128)(2,1)} %bitcast.1), calls=%async_computation.1 | async-start | bytes 327680 | tf_op jit(solution)/shard_map/all_to_all | solution.py:220
  79.1 0.6 copy-start
